TPU v7x, 256 devices: a whole 4x4x8 slice. The times are simulated.
256 devices in a mesh: dp: 16 (over y, x), tensor: 16 (over z, core).
Axes of the slice: x: 4, y: 4, z: 8, core: 2. Of those that a mesh axis runs over, the one named last changes fastest.
Arguments:
- tokens: bfloat16 [4096, 2048], P('dp'), may hold values from -6 to 6
- gate_weight: bfloat16 [8, 2048, 2816], P(None, 'dp', 'tensor'), may hold values from -0.25 to 0.25
- up_weight: bfloat16 [8, 2048, 2816], P(None, 'dp', 'tensor'), may hold values from -0.25 to 0.25
- down_weight: bfloat16 [8, 2816, 2048], P(None, 'tensor', 'dp'), may hold values from -0.3125 to 0.3125
- router_weight: float32 [2048, 8], replicated, may hold values from -6 to 6
- carry_mean: float32 [2048], replicated, may hold values from -0.375 to 0.375
Outputs:
- mixed: bfloat16 [4096, 2048], P(('dp', 'tensor'))
All inputs are finite; a program needn't handle non-finite values.
Results may differ from a plain program's by a relative error of at most 0.028.
Values may be sent and summed in bfloat16 or wider, within the bound.
A program may use at most 64 MiB of HBM per device.

v0:
```python
import jax
import jax.numpy as jnp
from jax import lax
from jax.sharding import PartitionSpec as P

SEG = 256
soft_cap = 8.0


def copy_for_each(array, axis):
    size = lax.axis_size(axis)
    return lax.all_to_all(
        jnp.broadcast_to(array[None], (size, *array.shape)), axis, 0, 0, tiled=True
    )


def joined_along(blocks, dim):
    blocks = jnp.moveaxis(blocks, 0, dim)
    lengths = blocks.shape
    return blocks.reshape(*lengths[:dim], lengths[dim] * lengths[dim + 1], *lengths[dim + 2 :])


def gather_directly(array, axis, dim):
    blocks = copy_for_each(array, axis)
    return joined_along(blocks, dim)


def split_up(array, dim, size):
    before, after = (array.shape[:dim], array.shape[dim + 1 :])
    return jnp.moveaxis(array.reshape(*before, size, -1, *after), dim, 0)


def sent_and_summed(array, axis, dim):
    size = lax.axis_size(axis)
    blocks = lax.all_to_all(split_up(array, dim, size), axis, 0, 0, tiled=True)
    return jnp.sum(blocks.astype(jnp.float32), axis=0)


def on_device(tokens, gate_weight, up_weight, down_weight, router_weight, carry_mean):
    dp_count = lax.axis_size("dp")
    tensor_count = lax.axis_size("tensor")
    own_rows, model_width = tokens.shape
    own_segs = own_rows // SEG
    all_segs = own_segs * dp_count
    experts, slice_rows, hidden_cols = gate_weight.shape
    own_means = jnp.sum(tokens.reshape(own_segs, SEG, model_width), axis=1, dtype=jnp.float32) / SEG
    own_logits = jnp.dot(
        own_means,
        router_weight,
        precision=lax.Precision.HIGHEST,
        preferred_element_type=jnp.float32,
    )
    seg_logits = gather_directly(own_logits, "dp", 0)
    carry_logits = jnp.dot(
        carry_mean[None, :],
        router_weight,
        precision=lax.Precision.HIGHEST,
        preferred_element_type=jnp.float32,
    )
    raw_logits = jnp.concatenate([carry_logits, seg_logits[:-1]], axis=0)
    logits = soft_cap * jnp.tanh(raw_logits / soft_cap)
    scores = jnp.exp(logits)
    probs_bf = (scores / jnp.sum(scores, axis=1, keepdims=True)).astype(jnp.bfloat16)
    gate_flat = gate_weight.reshape(experts, slice_rows * hidden_cols)
    up_flat = up_weight.reshape(experts, slice_rows * hidden_cols)
    merged_gate = jnp.dot(probs_bf, gate_flat, preferred_element_type=jnp.float32).astype(
        jnp.bfloat16
    )
    merged_up = jnp.dot(probs_bf, up_flat, preferred_element_type=jnp.float32).astype(jnp.bfloat16)
    merged_both = jnp.concatenate(
        [
            merged_gate.reshape(all_segs, slice_rows, hidden_cols),
            merged_up.reshape(all_segs, slice_rows, hidden_cols),
        ],
        axis=2,
    )
    full_rows = lax.all_to_all(merged_both, "dp", split_axis=0, concat_axis=1, tiled=True)
    own_tokens = tokens.reshape(own_segs, SEG, model_width)

    def add_block(block, total):
        rows_in = lax.dynamic_slice_in_dim(own_tokens, block * slice_rows, slice_rows, 2)
        weights_in = lax.dynamic_slice_in_dim(full_rows, block * slice_rows, slice_rows, 1)
        term = jnp.einsum("str,src->stc", rows_in, weights_in, preferred_element_type=jnp.float32)
        rounded = lax.optimization_barrier(term.astype(jnp.bfloat16))
        return total + rounded.astype(jnp.float32)

    start_total = jnp.zeros((own_segs, SEG, 2 * hidden_cols), jnp.float32)
    preact = lax.fori_loop(0, dp_count, add_block, start_total).reshape(own_rows, 2 * hidden_cols)
    hidden = (jax.nn.silu(preact[:, :hidden_cols]) * preact[:, hidden_cols:]).astype(jnp.bfloat16)
    down_cols = down_weight.shape[2]
    all_hidden = gather_directly(hidden, "dp", 0)
    merged_down = jnp.dot(
        probs_bf,
        down_weight.reshape(experts, hidden_cols * down_cols),
        preferred_element_type=jnp.float32,
    )
    merged_down = merged_down.astype(jnp.bfloat16).reshape(all_segs, hidden_cols, down_cols)
    partial_value = jnp.einsum(
        "stf,sfc->stc",
        all_hidden.reshape(all_segs, SEG, hidden_cols),
        merged_down,
        preferred_element_type=jnp.float32,
    )
    block_rows = own_rows // tensor_count
    partial_value = partial_value.reshape(dp_count, tensor_count, block_rows, down_cols)
    summed = sent_and_summed(partial_value.astype(jnp.bfloat16), "tensor", 1)
    moved = lax.all_to_all(
        summed.astype(jnp.bfloat16), "dp", split_axis=0, concat_axis=3, tiled=True
    )
    return moved.reshape(block_rows, dp_count * down_cols)


def solution(mesh):
    placed = (
        P("dp", None),
        P(None, "dp", "tensor"),
        P(None, "dp", "tensor"),
        P(None, "tensor", "dp"),
        P(),
        P(),
    )
    return jax.shard_map(
        on_device, mesh=mesh, in_specs=placed, out_specs=P(("dp", "tensor"), None), check_vma=False
    )
```

profile of v0, /device:TPU:1, one launch (start us, length us, event | category | flops | bytes accessed | tf_op | source)
XLA Modules:
  0.0 147.6 jit_solution(1069213658182428304)
XLA Ops:
  0.0 1.4 convert_reduce_fusion
  2.3 7.6 %all-to-all-start = ((f32[16,1,8]{2,1,0:T(1,128)}), f32[16,1,8]{2,1,0:T(1,128)S(1)}, u32[]{:S(2)}, u32[]{:S(2)}) async-start(f32[16,1,8]{2,1,0:T(1,128)} %broadcast_in_dim.7), calls=%async_computation | async-start | bytes 16384 | tf_op jit(solution)/shard_map/all_to_all | solution.py:12
  10.8 1.2 copy.21
  13.7 2.6 %all-to-all-done = f32[16,1,8]{2,1,0:T(1,128)S(1)} async-done(((f32[16,1,8]{2,1,0:T(1,128)}), f32[16,1,8]{2,1,0:T(1,128)S(1)}, u32[]{:S(2)}, u32[]{:S(2)}) %all-to-all-start) | async-done | bytes 544 | tf_op jit(solution)/shard_map/all_to_all | solution.py:12
  17.0 2.0 %reshape.81 = bf16[16,128,176]{2,1,0:T(8,128)(2,1)S(1)} reshape(bf16[16,22528]{1,0:T(8,128)(2,1)S(1)} %convolution_convert_fusion.3) | data formatting | bytes 1441792 | tf_op jit(solution)/shard_map/reshape | solution.py:72
  19.4 3.0 %reshape.83 = bf16[16,128,176]{2,1,0:T(8,128)(2,1)} reshape(bf16[16,22528]{1,0:T(8,128)(2,1)S(1)} %convolution_convert_fusion.2) | data formatting | bytes 1441792 | tf_op jit(solution)/shard_map/reshape | solution.py:73
  22.4 1.8 %pad_maximum_fusion = bf16[16,128,352]{2,1,0:T(8,128)(2,1)S(1)} fusion(bf16[16,128,176]{2,1,0:T(8,128)(2,1)} %reshape.83, bf16[16,128,176]{2,1,0:T(8,128)(2,1)S(1)} %reshape.81), kind=kLoop, calls=%fused_computation.12 | loop fusion | flops 2883584 | bytes 2883584 | tf_op jit(solution)/shard_map/concatenate | solution.py:70
  24.2 1.6 %copy.23 = bf16[16,128,352]{1,2,0:T(8,128)(2,1)} copy(bf16[16,128,352]{2,1,0:T(8,128)(2,1)S(1)} %pad_maximum_fusion) | data formatting | bytes 2883584 | tf_op jit(solution)/shard_map/concatenate | solution.py:70
  25.9 4.1 %all-to-all-start.1 = ((bf16[16,128,352]{1,2,0:T(8,128)(2,1)}), bf16[16,128,352]{1,2,0:T(8,128)(2,1)S(1)}, u32[]{:S(2)}, u32[]{:S(2)}) async-start(bf16[16,128,352]{1,2,0:T(8,128)(2,1)} %copy.23), calls=%async_computation.1 | async-start | bytes 2883584 | tf_op jit(solution)/shard_map/all_to_all | solution.py:77
  30.0 19.5 %all-to-all-done.1 = bf16[16,128,352]{1,2,0:T(8,128)(2,1)S(1)} async-done(((bf16[16,128,352]{1,2,0:T(8,128)(2,1)}), bf16[16,128,352]{1,2,0:T(8,128)(2,1)S(1)}, u32[]{:S(2)}, u32[]{:S(2)}) %all-to-all-start.1) | async-done | bytes 1441824 | tf_op jit(solution)/shard_map/all_to_all | solution.py:77
  50.3 19.8 %while.14 = (s32[]{:T(128)}, f32[1,256,352]{1,2,0:T(8,128)S(1)}, bf16[1,256,2048]{2,1,0:T(8,128)(2,1)}, bf16[1,2048,352]{2,1,0:T(8,128)(2,1)S(1)}, s32[]{:T(128)}, /*index=5*/s32[]{:T(128)}, s32[]{:T(128)}, s32[]{:T(128)}) while((s32[]{:T(128)}, f32[1,256,352]{1,2,0:T(8,128)S(1)}, bf16[1,256,2048]{2,1,0:T(8,128)(2,1)}, ...), condition=%wide.region_3.0_spmd.clone, body=%wide.region_2.0_spmd.clone.sunk | while | flops 23429124 | bytes 1246349 | solution.py:88
  50.3 1.1 fusion.31
  51.6 1.1 fusion.31
  55.3 1.1 fusion.31
  56.5 1.1 fusion.31
  57.8 1.1 fusion.31
  60.3 1.1 fusion.31
  62.8 1.1 fusion.31
  66.5 1.1 fusion.31
  70.3 1.2 broadcast_in_dim.8
  71.5 5.5 %all-to-all-start.2 = ((bf16[16,256,176]{1,2,0:T(8,128)(2,1)}), bf16[16,256,176]{1,2,0:T(8,128)(2,1)S(1)}, u32[]{:S(2)}, u32[]{:S(2)}) async-start(bf16[16,256,176]{1,2,0:T(8,128)(2,1)} %broadcast_in_dim.8), calls=%async_computation.2 | async-start | bytes 2883584 | tf_op jit(solution)/shard_map/all_to_all | solution.py:12
  77.5 18.8 %all-to-all-done.2 = bf16[16,256,176]{1,2,0:T(8,128)(2,1)S(1)} async-done(((bf16[16,256,176]{1,2,0:T(8,128)(2,1)}), bf16[16,256,176]{1,2,0:T(8,128)(2,1)S(1)}, u32[]{:S(2)}, u32[]{:S(2)}) %all-to-all-start.2) | async-done | bytes 1441824 | tf_op jit(solution)/shard_map/all_to_all | solution.py:12
  97.3 40.4 %all_to_all.42 = bf16[16,16,1,16,128]{4,3,1,2,0:T(8,128)(2,1)S(1)} all-to-all(bf16[16,16,1,16,128]{4,3,1,2,0:T(8,128)(2,1)S(1)} %bitcast.58), channel_id=1, replica_groups=mesh['dp'=16,'tensor'=16] {'tensor'}, dimensions={0} | all-to-all | bytes 2097152 | tf_op jit(solution)/shard_map/all_to_all | solution.py:35
  137.8 9.1 %all_to_all.43 = bf16[16,1,16,128]{3,2,1,0:T(8,128)(2,1)S(1)} all-to-all(bf16[16,1,16,128]{3,2,1,0:T(8,128)(2,1)S(1)} %bitcast.63), channel_id=1, replica_groups=mesh['dp'=16,'tensor'=16] {'dp'}, dimensions={0} | all-to-all | bytes 131072 | tf_op jit(solution)/shard_map/all_to_all | solution.py:107
  (53 shorter events, 18.1 us)
Async XLA Ops:
  0.0 1.5 copy-start
  0.0 12.8 %copy-start.1 = (bf16[8,128,176]{1,2,0:T(8,128)(2,1)S(1)}, bf16[8,128,176]{1,2,0:T(8,128)(2,1)}, u32[]{:S(2)}) copy-start(bf16[8,128,176]{1,2,0:T(8,128)(2,1)} %param.10) | copy-start | bytes 1081348
  2.3 13.9 %all-to-all-start = ((f32[16,1,8]{2,1,0:T(1,128)}), f32[16,1,8]{2,1,0:T(1,128)S(1)}, u32[]{:S(2)}, u32[]{:S(2)}) async-start(f32[16,1,8]{2,1,0:T(1,128)} %broadcast_in_dim.7), calls=%async_computation | async-start | bytes 16384 | tf_op jit(solution)/shard_map/all_to_all | solution.py:12
  25.9 23.6 %all-to-all-start.1 = ((bf16[16,128,352]{1,2,0:T(8,128)(2,1)}), bf16[16,128,352]{1,2,0:T(8,128)(2,1)S(1)}, u32[]{:S(2)}, u32[]{:S(2)}) async-start(bf16[16,128,352]{1,2,0:T(8,128)(2,1)} %copy.23), calls=%async_computation.1 | async-start | bytes 2883584 | tf_op jit(solution)/shard_map/all_to_all | solution.py:77
  71.5 5.5 %copy-start.2 = (bf16[8,176,128]{2,1,0:T(8,128)(2,1)S(1)}, bf16[8,176,128]{2,1,0:T(8,128)(2,1)}, u32[]{:S(2)}) copy-start(bf16[8,176,128]{2,1,0:T(8,128)(2,1)} %param.11) | copy-start | bytes 1081348
  71.5 24.7 %all-to-all-start.2 = ((bf16[16,256,176]{1,2,0:T(8,128)(2,1)}), bf16[16,256,176]{1,2,0:T(8,128)(2,1)S(1)}, u32[]{:S(2)}, u32[]{:S(2)}) async-start(bf16[16,256,176]{1,2,0:T(8,128)(2,1)} %broadcast_in_dim.8), calls=%async_computation.2 | async-start | bytes 2883584 | tf_op jit(solution)/shard_map/all_to_all | solution.py:12
where the time goes:
time: 149 us; the launch traced here: 148 us
  blocking collectives  49.5 us (33%)
  waiting for transfers between devices  40.8 us (27%)
  matrix products  20.7 us (14%)
  starting transfers between devices  17.1 us (11%)
  local copies, waits for them, and re-layouts  13.3 us (9%)
  other arithmetic  5.29 us (4%)
    all_to_all x1, blocking collectives, sent_and_summed(): blocks = lax.all_to_all(split_up(array, dim, size), axis, 0, 0, tiled=True)  40.4 us
    all_to_all x2, waiting for transfers between devices, copy_for_each(): lax.all_to_all(jnp.broadcast_to(array[None], (size, *array.shape)), axis,...  21.3 us
    all_to_all x1, waiting for transfers between devices, on_device(): lax.all_to_all(merged_both, 'dp', split_axis=0, concat_axis=1, tiled=True)  19.5 us
    dot_general x16, matrix products, add_block(): jnp.einsum('str,src->stc', rows_in, weights_in, preferred_element_type=jn...  17.6 us
    all_to_all x2, starting transfers between devices, copy_for_each(): lax.all_to_all(jnp.broadcast_to(array[None], (size, *array.shape)), axis,...  13 us
    all_to_all x1, blocking collectives, on_device(): lax.all_to_all(summed.astype(jnp.bfloat16), 'dp', split_axis=0, concat_ax...  9.07 us
    all_to_all x1, starting transfers between devices, on_device(): lax.all_to_all(merged_both, 'dp', split_axis=0, concat_axis=1, tiled=True)  4.09 us
    unnamed x12, local copies, waits for them, and re-layouts  3.14 us
  transfers between devices with their start and end apart: 3, of which 3 were waited for; matrix products, arithmetic and copies ran while one was open for 3% of the time, Pallas kernels for 0%

commit v1 on v0

--- a/solution.py
+++ b/solution.py
@@ -104,8 +104,14 @@
     block_rows = own_rows // tensor_count
     partial_value = partial_value.reshape(dp_count, tensor_count, block_rows, down_cols)
     summed = sent_and_summed(partial_value.astype(jnp.bfloat16), "tensor", 1)
-    moved = lax.all_to_all(
-        summed.astype(jnp.bfloat16), "dp", split_axis=0, concat_axis=3, tiled=True
+    moved = jnp.concatenate(
+        lax.all_to_all(
+            jnp.stack(jnp.split(summed.astype(jnp.bfloat16), lax.axis_size("dp"), axis=0)),
+            "dp",
+            0,
+            0,
+        ),
+        axis=3,
     )
     return moved.reshape(block_rows, dp_count * down_cols)
 

time: 149 us -> 149 us (level)
    unnamed x12 -> x27, local copies, waits for them, and re-layouts: 3.14 us -> 3.27 us
where the time goes in v1:
time: 149 us; the launch traced here: 148 us
  blocking collectives  49.5 us (33%)
  waiting for transfers between devices  40.8 us (27%)
  matrix products  20.7 us (14%)
  starting transfers between devices  17.1 us (11%)
  local copies, waits for them, and re-layouts  13.5 us (9%)
  other arithmetic  5.29 us (4%)
    all_to_all x1, blocking collectives, sent_and_summed(): blocks = lax.all_to_all(split_up(array, dim, size), axis, 0, 0, tiled=True)  40.4 us
    all_to_all x2, waiting for transfers between devices, copy_for_each(): lax.all_to_all(jnp.broadcast_to(array[None], (size, *array.shape)), axis,...  21.3 us
    all_to_all x1, waiting for transfers between devices, on_device(): lax.all_to_all(merged_both, 'dp', split_axis=0, concat_axis=1, tiled=True)  19.5 us
    dot_general x16, matrix products, add_block(): jnp.einsum('str,src->stc', rows_in, weights_in, preferred_element_type=jn...  17.6 us
    all_to_all x2, starting transfers between devices, copy_for_each(): lax.all_to_all(jnp.broadcast_to(array[None], (size, *array.shape)), axis,...  13 us
    all_to_all x1, blocking collectives, on_device(): lax.all_to_all(jnp.stack(jnp.split(summed.astype(jnp.bfloat16), lax.axis_...  9.07 us
    all_to_all x1, starting transfers between devices, on_device(): lax.all_to_all(merged_both, 'dp', split_axis=0, concat_axis=1, tiled=True)  4.09 us
    unnamed x27, local copies, waits for them, and re-layouts  3.27 us
  transfers between devices with their start and end apart: 3, of which 3 were waited for; matrix products, arithmetic and copies ran while one was open for 3% of the time, Pallas kernels for 0%

profile of v1, /device:TPU:1, one launch (start us, length us, event | category | flops | bytes accessed | tf_op | source)
XLA Modules:
  0.0 147.8 jit_solution(15012829841106230794)
XLA Ops:
  0.0 1.4 convert_reduce_fusion
  2.3 7.6 %all-to-all-start = ((f32[16,1,8]{2,1,0:T(1,128)}), f32[16,1,8]{2,1,0:T(1,128)S(1)}, u32[]{:S(2)}, u32[]{:S(2)}) async-start(f32[16,1,8]{2,1,0:T(1,128)} %broadcast_in_dim.7), calls=%async_computation | async-start | bytes 16384 | tf_op jit(solution)/shard_map/all_to_all | solution.py:12
  10.8 1.2 copy.39
  13.7 2.6 %all-to-all-done = f32[16,1,8]{2,1,0:T(1,128)S(1)} async-done(((f32[16,1,8]{2,1,0:T(1,128)}), f32[16,1,8]{2,1,0:T(1,128)S(1)}, u32[]{:S(2)}, u32[]{:S(2)}) %all-to-all-start) | async-done | bytes 544 | tf_op jit(solution)/shard_map/all_to_all | solution.py:12
  17.0 2.0 %reshape.112 = bf16[16,128,176]{2,1,0:T(8,128)(2,1)S(1)} reshape(bf16[16,22528]{1,0:T(8,128)(2,1)S(1)} %convolution_convert_fusion.3) | data formatting | bytes 1441792 | tf_op jit(solution)/shard_map/reshape | solution.py:72
  19.4 3.0 %reshape.114 = bf16[16,128,176]{2,1,0:T(8,128)(2,1)} reshape(bf16[16,22528]{1,0:T(8,128)(2,1)S(1)} %convolution_convert_fusion.2) | data formatting | bytes 1441792 | tf_op jit(solution)/shard_map/reshape | solution.py:73
  22.4 1.8 %pad_maximum_fusion = bf16[16,128,352]{2,1,0:T(8,128)(2,1)S(1)} fusion(bf16[16,128,176]{2,1,0:T(8,128)(2,1)} %reshape.114, bf16[16,128,176]{2,1,0:T(8,128)(2,1)S(1)} %reshape.112), kind=kLoop, calls=%fused_computation.12 | loop fusion | flops 2883584 | bytes 2883584 | tf_op jit(solution)/shard_map/concatenate | solution.py:70
  24.2 1.6 %copy.41 = bf16[16,128,352]{1,2,0:T(8,128)(2,1)} copy(bf16[16,128,352]{2,1,0:T(8,128)(2,1)S(1)} %pad_maximum_fusion) | data formatting | bytes 2883584 | tf_op jit(solution)/shard_map/concatenate | solution.py:70
  25.9 4.1 %all-to-all-start.1 = ((bf16[16,128,352]{1,2,0:T(8,128)(2,1)}), bf16[16,128,352]{1,2,0:T(8,128)(2,1)S(1)}, u32[]{:S(2)}, u32[]{:S(2)}) async-start(bf16[16,128,352]{1,2,0:T(8,128)(2,1)} %copy.41), calls=%async_computation.1 | async-start | bytes 2883584 | tf_op jit(solution)/shard_map/all_to_all | solution.py:77
  30.0 19.5 %all-to-all-done.1 = bf16[16,128,352]{1,2,0:T(8,128)(2,1)S(1)} async-done(((bf16[16,128,352]{1,2,0:T(8,128)(2,1)}), bf16[16,128,352]{1,2,0:T(8,128)(2,1)S(1)}, u32[]{:S(2)}, u32[]{:S(2)}) %all-to-all-start.1) | async-done | bytes 1441824 | tf_op jit(solution)/shard_map/all_to_all | solution.py:77
  50.3 19.8 %while.14 = (s32[]{:T(128)}, f32[1,256,352]{1,2,0:T(8,128)S(1)}, bf16[1,256,2048]{2,1,0:T(8,128)(2,1)}, bf16[1,2048,352]{2,1,0:T(8,128)(2,1)S(1)}, s32[]{:T(128)}, /*index=5*/s32[]{:T(128)}, s32[]{:T(128)}, s32[]{:T(128)}) while((s32[]{:T(128)}, f32[1,256,352]{1,2,0:T(8,128)S(1)}, bf16[1,256,2048]{2,1,0:T(8,128)(2,1)}, ...), condition=%wide.region_3.0_spmd.clone, body=%wide.region_2.0_spmd.clone.sunk | while | flops 23429124 | bytes 1246349 | solution.py:88
  50.3 1.1 fusion.31
  51.6 1.1 fusion.31
  55.3 1.1 fusion.31
  56.5 1.1 fusion.31
  57.8 1.1 fusion.31
  60.3 1.1 fusion.31
  62.8 1.1 fusion.31
  66.5 1.1 fusion.31
  70.3 1.2 broadcast_in_dim.8
  71.5 5.5 %all-to-all-start.2 = ((bf16[16,256,176]{1,2,0:T(8,128)(2,1)}), bf16[16,256,176]{1,2,0:T(8,128)(2,1)S(1)}, u32[]{:S(2)}, u32[]{:S(2)}) async-start(bf16[16,256,176]{1,2,0:T(8,128)(2,1)} %broadcast_in_dim.8), calls=%async_computation.2 | async-start | bytes 2883584 | tf_op jit(solution)/shard_map/all_to_all | solution.py:12
  77.5 18.8 %all-to-all-done.2 = bf16[16,256,176]{1,2,0:T(8,128)(2,1)S(1)} async-done(((bf16[16,256,176]{1,2,0:T(8,128)(2,1)}), bf16[16,256,176]{1,2,0:T(8,128)(2,1)S(1)}, u32[]{:S(2)}, u32[]{:S(2)}) %all-to-all-start.2) | async-done | bytes 1441824 | tf_op jit(solution)/shard_map/all_to_all | solution.py:12
  97.3 40.4 %all_to_all.32 = bf16[16,16,1,16,128]{4,3,1,2,0:T(8,128)(2,1)S(1)} all-to-all(bf16[16,16,1,16,128]{4,3,1,2,0:T(8,128)(2,1)S(1)} %bitcast.117), channel_id=1, replica_groups=mesh['dp'=16,'tensor'=16] {'tensor'}, dimensions={0} | all-to-all | bytes 2097152 | tf_op jit(solution)/shard_map/all_to_all | solution.py:35
  138.0 9.1 %all_to_all.33 = bf16[16,1,1,16,128]{4,3,2,1,0:T(8,128)(2,1)S(1)} all-to-all(bf16[16,1,1,16,128]{4,3,2,1,0:T(8,128)(2,1)S(1)} %constant_dynamic-update-slice_fusion), channel_id=1, replica_groups=mesh['dp'=16,'tensor'=16] {'dp'}, dimensions={0} | all-to-all | bytes 131072 | tf_op jit(solution)/shard_map/all_to_all | solution.py:108
  (69 shorter events, 18.3 us)
Async XLA Ops:
  0.0 1.5 copy-start
  0.0 12.8 %copy-start.1 = (bf16[8,128,176]{1,2,0:T(8,128)(2,1)S(1)}, bf16[8,128,176]{1,2,0:T(8,128)(2,1)}, u32[]{:S(2)}) copy-start(bf16[8,128,176]{1,2,0:T(8,128)(2,1)} %param.10) | copy-start | bytes 1081348
  2.3 13.9 %all-to-all-start = ((f32[16,1,8]{2,1,0:T(1,128)}), f32[16,1,8]{2,1,0:T(1,128)S(1)}, u32[]{:S(2)}, u32[]{:S(2)}) async-start(f32[16,1,8]{2,1,0:T(1,128)} %broadcast_in_dim.7), calls=%async_computation | async-start | bytes 16384 | tf_op jit(solution)/shard_map/all_to_all | solution.py:12
  25.9 23.6 %all-to-all-start.1 = ((bf16[16,128,352]{1,2,0:T(8,128)(2,1)}), bf16[16,128,352]{1,2,0:T(8,128)(2,1)S(1)}, u32[]{:S(2)}, u32[]{:S(2)}) async-start(bf16[16,128,352]{1,2,0:T(8,128)(2,1)} %copy.41), calls=%async_computation.1 | async-start | bytes 2883584 | tf_op jit(solution)/shard_map/all_to_all | solution.py:77
  71.5 5.5 %copy-start.2 = (bf16[8,176,128]{2,1,0:T(8,128)(2,1)S(1)}, bf16[8,176,128]{2,1,0:T(8,128)(2,1)}, u32[]{:S(2)}) copy-start(bf16[8,176,128]{2,1,0:T(8,128)(2,1)} %param.11) | copy-start | bytes 1081348
  71.5 24.7 %all-to-all-start.2 = ((bf16[16,256,176]{1,2,0:T(8,128)(2,1)}), bf16[16,256,176]{1,2,0:T(8,128)(2,1)S(1)}, u32[]{:S(2)}, u32[]{:S(2)}) async-start(bf16[16,256,176]{1,2,0:T(8,128)(2,1)} %broadcast_in_dim.8), calls=%async_computation.2 | async-start | bytes 2883584 | tf_op jit(solution)/shard_map/all_to_all | solution.py:12
